TPU v7x, 64 devices: a 2x2x8 block of a 4x4x8 slice. The times are simulated.
64 devices in a mesh: dp: 4 (over x, y), ep: 16 (over z, core).
Axes of the slice: x: 2, y: 2, z: 8, core: 2. Of those that a mesh axis runs over, the one named last changes fastest.
The devices are a block of a 4x4x8 slice.
Arguments:
- dispatched: bfloat16 [64, 64, 32, 2048], P('dp', 'ep'), parts along dimension 0
- w_gate: bfloat16 [64, 2048, 1024], P('ep')
- w_up: bfloat16 [64, 2048, 1024], P('ep')
- w_down: bfloat16 [64, 1024, 2048], P('ep')
- fill_count: int32 [64, 64], P('dp', 'ep'), parts along dimension 0
- slot_index: int32 [8192, 8], P(('dp', 'ep')), parts along dimension 0
- expert_id: int32 [8192, 8], P(('dp', 'ep')), parts along dimension 0
- gate_weight: float32 [8192, 8], P(('dp', 'ep')), parts along dimension 0
Outputs:
- output: bfloat16 [8192, 2048], P(('dp', 'ep')), parts along dimension 0
There are 4 independent parts. A program takes and returns all parts, laid end to end along the dimension named above; an argument that names none is the same for every part.
All inputs are finite; a program needn't handle non-finite values.
Results may differ from a plain program's by a relative error of at most 0.00122.
Values are sent between devices in bfloat16 or wider.
A program may use at most 768 MiB of HBM per device.

v0:
```python
import jax
import jax.numpy as jnp
from jax import lax
from jax.sharding import PartitionSpec as P


def expert_rows(dispatched, w_gate, w_up, w_down, fill_count):
    capacity = dispatched.shape[2]
    pre_gate = jnp.einsum("secd,edf->escf", dispatched, w_gate, preferred_element_type=jnp.float32)
    pre_up = jnp.einsum("secd,edf->escf", dispatched, w_up, preferred_element_type=jnp.float32)
    hidden = (jax.nn.silu(pre_gate) * pre_up).astype(jnp.bfloat16)
    result = jnp.einsum("escf,efd->escd", hidden, w_down, preferred_element_type=jnp.float32).astype(jnp.bfloat16)
    live_mask = jnp.arange(capacity)[None, None, :] < fill_count.T[:, :, None]
    return jnp.where(live_mask[..., None], result, 0)


def solution(mesh):
    def local_step(dispatched, w_gate, w_up, w_down, fill_count, slot_index, expert_id, gate_weight):
        result = expert_rows(dispatched, w_gate, w_up, w_down, fill_count)
        returned = lax.all_to_all(result, "ep", 1, 0, tiled=True)
        flat_rows = returned.reshape(-1, returned.shape[-1])
        row_index = expert_id * dispatched.shape[2] + jnp.maximum(slot_index, 0)
        picked = jnp.take(flat_rows, row_index, axis=0)
        weight = jnp.where(slot_index >= 0, gate_weight, 0.0)
        combined = jnp.sum(weight[:, :, None] * picked.astype(jnp.float32), axis=1)
        return combined.astype(jnp.bfloat16)
    token_spec = P(("dp", "ep"))
    in_specs = (P("dp", "ep"), P("ep"), P("ep"), P("ep"), P("dp", "ep"), token_spec, token_spec, token_spec)
    return jax.shard_map(local_step, mesh=mesh, in_specs=in_specs, out_specs=token_spec, check_vma=False)
```

profile of v0, /device:TPU:30, one launch (start us, length us, event | category | flops | bytes accessed | tf_op | source)
XLA Modules:
  0.0 280.8 jit_solution(14667206585128922726)
XLA Ops:
  0.0 0.8 iota_compare_fusion
  0.8 17.0 %fusion.2 = f32[4,16,32,1024]{3,2,1,0:T(8,128)} fusion(bf16[4,2048,1024]{2,1,0:T(8,128)(2,1)} %param.10, bf16[16,4,32,2048]{3,2,1,0:T(8,128)(2,1)} %param.8), kind=kOutput, calls=%fused_computation.3 | convolution fusion | flops 8589934592 | bytes 33554432 | tf_op jit(solution)/shard_map/secd,edf->escf/dot_general | solution.py:10
  17.8 19.3 %multiply_convert_fusion = bf16[4,16,32,1024]{3,2,1,0:T(8,128)(2,1)} fusion(f32[4,16,32,1024]{3,2,1,0:T(8,128)} %fusion.2, bf16[4,2048,1024]{2,1,0:T(8,128)(2,1)} %param.9, bf16[16,4,32,2048]{3,2,1,0:T(8,128)(2,1)} %param.8), kind=kOutput, calls=%fused_computation.9 | convolution fusion | flops 8602517504 | bytes 37748736 | tf_op jit(solution)/shard_map/secd,edf->escf/dot_general | solution.py:9
  37.0 17.5 %convert_select_fusion = bf16[4,16,32,2048]{3,2,1,0:T(8,128)(2,1)} fusion(pred[4,16,32]{2,1,0:T(8,128)(4,1)S(1)} %iota_compare_fusion, bf16[4,16,32,1024]{3,2,1,0:T(8,128)(2,1)} %multiply_convert_fusion, bf16[4,1024,2048]{2,1,0:T(8,128)(2,1)} %param.11), kind=kOutput, calls=%fused_computation.8 | convolution fusion | flops 8598323200 | bytes 29362176 | tf_op jit(solution)/shard_map/escf,efd->escd/dot_general | solution.py:12
  54.5 8.3 %copy.21 = bf16[4,16,32,2048]{3,2,0,1:T(8,128)(2,1)} copy(bf16[4,16,32,2048]{3,2,1,0:T(8,128)(2,1)} %convert_select_fusion) | data formatting | bytes 16777216 | tf_op jit(solution)/shard_map/jit(_where)/select_n | solution.py:14
  62.8 0.0 copy-start
  62.8 0.0 copy-start.2
  62.8 0.0 copy-start.1
  62.8 9.7 %all-to-all-start = ((bf16[4,16,32,2048]{3,2,0,1:T(8,128)(2,1)}), bf16[4,16,32,2048]{3,2,0,1:T(8,128)(2,1)}, u32[]{:S(2)}, u32[]{:S(2)}) async-start(bf16[4,16,32,2048]{3,2,0,1:T(8,128)(2,1)} %copy.21), calls=%async_computation | async-start | bytes 16777216 | tf_op jit(solution)/shard_map/all_to_all | solution.py:20
  72.5 0.0 copy-done
  72.5 0.0 copy-done.2
  72.6 0.1 copy.22
  72.7 0.1 reshape.18
  72.8 0.0 copy-done.1
  72.8 0.1 copy.17
  72.9 0.1 copy.18
  73.0 188.3 %all-to-all-done = bf16[4,16,32,2048]{3,2,0,1:T(8,128)(2,1)} async-done(((bf16[4,16,32,2048]{3,2,0,1:T(8,128)(2,1)}), bf16[4,16,32,2048]{3,2,0,1:T(8,128)(2,1)}, u32[]{:S(2)}, u32[]{:S(2)}) %all-to-all-start) | async-done | bytes 8388640 | tf_op jit(solution)/shard_map/all_to_all | solution.py:20
  261.3 13.3 %gather_fusion = bf16[1024,2048]{1,0:T(8,128)(2,1)} fusion(bf16[2048,2048]{1,0:T(8,128)(2,1)} %bitcast.9, s32[1024]{0:T(1024)S(1)} %broadcast_clamp_fusion), kind=kCustom, calls=%fused_computation | custom fusion | bytes 8392704 | tf_op jit(solution)/shard_map/jit(_take)/gather | solution.py:23
  274.5 6.3 %multiply_reduce_fusion = bf16[128,2048]{1,0:T(8,128)(2,1)} fusion(bf16[1024,2048]{1,0:T(8,128)(2,1)} %gather_fusion, f32[128,8]{1,0:T(8,128)S(1)} %copy.17, pred[128,8]{1,0:T(8,128)(4,1)S(1)} %copy.18), kind=kLoop, calls=%fused_computation.7 | loop fusion | flops 8126464 | bytes 4723712 | tf_op jit(solution)/shard_map/reduce_sum | solution.py:25
  (3 shorter events, 0.0 us)
Async XLA Ops:
  62.8 9.7 %copy-start = (s32[128,8]{0,1:T(8,128)S(1)}, s32[128,8]{0,1:T(8,128)}, u32[]{:S(2)}) copy-start(s32[128,8]{0,1:T(8,128)} %param.13) | copy-start | bytes 12292
  62.8 9.8 %copy-start.2 = (s32[128,8]{0,1:T(8,128)S(1)}, s32[128,8]{0,1:T(8,128)}, u32[]{:S(2)}) copy-start(s32[128,8]{0,1:T(8,128)} %param.14) | copy-start | bytes 12292
  62.8 10.0 %copy-start.1 = (f32[128,8]{0,1:T(8,128)S(1)}, f32[128,8]{0,1:T(8,128)}, u32[]{:S(2)}) copy-start(f32[128,8]{0,1:T(8,128)} %param.15) | copy-start | bytes 12292
  62.8 198.5 %all-to-all-start = ((bf16[4,16,32,2048]{3,2,0,1:T(8,128)(2,1)}), bf16[4,16,32,2048]{3,2,0,1:T(8,128)(2,1)}, u32[]{:S(2)}, u32[]{:S(2)}) async-start(bf16[4,16,32,2048]{3,2,0,1:T(8,128)(2,1)} %copy.21), calls=%async_computation | async-start | bytes 16777216 | tf_op jit(solution)/shard_map/all_to_all | solution.py:20
where the time goes:
time: 282 us; the launch traced here: 281 us
  waiting for transfers between devices  188 us (67%)
  matrix products  53.7 us (19%)
  local copies, waits for them, and re-layouts  22 us (8%)
  starting transfers between devices  9.73 us (3%)
  other arithmetic  7.05 us (2%)
    all_to_all x1, waiting for transfers between devices, local_step(): returned = lax.all_to_all(result, 'ep', 1, 0, tiled=True)  188 us
    dot_general x1, matrix products, expert_rows(): jnp.einsum('secd,edf->escf', dispatched, w_gate, preferred_element_type=j...  19.3 us
    dot_general x1, matrix products, expert_rows(): jnp.einsum('escf,efd->escd', hidden, w_down, preferred_element_type=jnp.f...  17.5 us
    dot_general x1, matrix products, expert_rows(): jnp.einsum('secd,edf->escf', dispatched, w_up, preferred_element_type=jnp...  17 us
    gather x1, local copies, waits for them, and re-layouts, local_step(): picked = jnp.take(flat_rows, row_index, axis=0)  13.3 us
    all_to_all x1, starting transfers between devices, local_step(): returned = lax.all_to_all(result, 'ep', 1, 0, tiled=True)  9.73 us
    select_n x1, local copies, waits for them, and re-layouts, expert_rows(): return jnp.where(live_mask[..., None], result, 0)  8.27 us
    reduce_sum x1, other arithmetic, local_step(): combined = jnp.sum(weight[:, :, None] * picked.astype(jnp.float32), axis=1)  6.27 us
  transfers between devices with their start and end apart: 1, of which 1 were waited for; matrix products, arithmetic and copies ran while one was open for 0% of the time, Pallas kernels for 0%

commit v1 on v0

v1 whole, which is shorter than its diff:
```python
import functools

import jax
import jax.numpy as jnp
from jax import lax
from jax.experimental import pallas as pl
from jax.experimental.pallas import tpu as pltpu
from jax.sharding import PartitionSpec as P

MESH = pl.DeviceIdType.MESH
BLOCKS_A = ((4, 0), (-3, 0), (4, 1), (-3, 1), (3, 0), (-2, 0), (3, 1), (-2, 1))
BLOCKS_B = (((2, 0), (-1, 0), (2, 1), (-1, 1)), ((1, 0), (0, 0), (1, 1), (0, 1)))
CLASS = {3: 0, -2: 1, 2: 2, -1: 3, 1: 4, 0: 5}
LEAF = 4
TILE = 512


def kernel(zn, disp, wg, wu, wd, fill, slot, eid, gw, out,
           xa, xb, wgb, wub, wdb, hid, lsend, leaf, ysend, ybuf, head, part, meta, scr, sel,
           xa_sem, xb_sem, w_sem, lsend_sem, leaf_sem, ysend_sem, ybuf_sem, psend_sem, part_sem, msend_sem, meta_sem):
    me = lax.axis_index("ep")
    z, k = me // 2, lax.rem(me, 2)
    sigma = 1 - 2 * k
    experts, cap, dim = disp.shape[1:]
    ffn = wg.shape[2]
    tokens, top_k = slot.shape
    per_core = experts * cap
    chunks, _, width = part.shape[1:]
    units = 3 * experts

    def dev(a, rel):
        chip = lax.rem(z + a * sigma + zn, zn) if rel == 0 else lax.rem(z - a * sigma + zn, zn)
        return 2 * chip + (k if rel == 0 else 1 - k)

    def remote(src, dst, send, recv, target):
        return pltpu.make_async_remote_copy(src_ref=src, dst_ref=dst, send_sem=send, recv_sem=recv,
                                            device_id={"ep": target}, device_id_type=MESH)

    def rows_of(core, e):
        return pl.ds(pl.multiple_of(core * per_core + e * cap, cap), cap)

    def rows_meta(cls):
        return pl.ds(2 * top_k * cls, 2 * top_k)

    def xa_copy(e, b):
        return pltpu.make_async_copy(disp.at[dev(*BLOCKS_A[b]), e], xa.at[e, pl.ds(b * cap, cap)], xa_sem.at[e, b])

    def xb_copy(p, e, b):
        return pltpu.make_async_copy(disp.at[dev(*BLOCKS_B[p][b]), e], xb.at[p, e, pl.ds(b * cap, cap)],
                                     xb_sem.at[p, e, b])

    def w_copy(which, u):
        src, dst = ((wg, wgb), (wu, wub), (wd, wdb))[which]
        return pltpu.make_async_copy(src.at[lax.rem(u, experts)], dst.at[lax.rem(u, 2)], w_sem.at[which, lax.rem(u, 2)])

    def start_xa(e):
        for b in range(len(BLOCKS_A)):
            xa_copy(e, b).start()

    def start_xb(p, e):
        for b in range(len(BLOCKS_B[p])):
            xb_copy(p, e, b).start()

    for u in range(2):
        start_xa(u)
        for which in range(3):
            w_copy(which, u).start()

    scr[...] = jnp.zeros_like(scr)
    flat = jnp.where(slot[...] >= 0, eid[...] * cap + slot[...], -1)
    scr[:, 0:top_k] = flat.astype(jnp.float32)
    scr[:, top_k:2 * top_k] = gw[...]
    own = scr[...].T
    meta[...] = jnp.zeros_like(meta)
    meta[rows_meta(CLASS[0])] = own[0:2 * top_k]

    barrier = pltpu.get_barrier_semaphore()
    partners = [(0, 1), (1, 0), (-1, 0), (1, 1), (-1, 1), (2, 0), (-2, 0), (3, 0), (-3, 0)]
    for a, rel in partners:
        pl.semaphore_signal(barrier, inc=1, device_id={"ep": dev(a, rel)}, device_id_type=MESH)
    pl.semaphore_wait(barrier, len(partners))
    meta_to = [(-3, 0), (2, 1), (-2, 2), (1, 3), (-1, 4)]

    def meta_copy(a, cls):
        return remote(meta.at[rows_meta(CLASS[0])], meta.at[rows_meta(cls)], msend_sem.at[cls], meta_sem.at[cls], dev(a, 0))

    for a, cls in meta_to:
        meta_copy(a, cls).start()

    def up_phase(x_ref, e, u, blocks):
        s = lax.rem(u, 2)
        row = lax.broadcasted_iota(jnp.int32, (cap, TILE), 0)

        def tile(n, carry):
            cols = pl.ds(pl.multiple_of(n * TILE, TILE), TILE)
            x = x_ref[...]
            a = jnp.dot(x, wgb[s, :, cols], preferred_element_type=jnp.float32)
            b = jnp.dot(x, wub[s, :, cols], preferred_element_type=jnp.float32)
            h = jax.nn.silu(a) * b
            for i, block in enumerate(blocks):
                live = row < fill[dev(*block), e]
                hid[i * cap:(i + 1) * cap, cols] = jnp.where(live, h[i * cap:(i + 1) * cap], 0.0).astype(jnp.bfloat16)
            return carry

        lax.fori_loop(0, ffn // TILE, tile, 0)

    def down_phase(e, u, blocks, first):
        s = lax.rem(u, 2)
        rows = len(blocks) * cap

        def tile(n, carry):
            cols = pl.ds(pl.multiple_of(n * TILE, TILE), TILE)
            y = jnp.dot(hid[0:rows], wdb[s, :, cols], preferred_element_type=jnp.float32).astype(jnp.bfloat16)
            for i, (a, rel) in enumerate(blocks):
                block = y[i * cap:(i + 1) * cap]
                if first and i < LEAF:
                    lsend[i, e, :, cols] = block
                elif rel == 0:
                    ybuf[CLASS[a], rows_of(0, e), cols] = block
                else:
                    ysend[CLASS[a], e, :, cols] = block
            return carry

        lax.fori_loop(0, dim // TILE, tile, 0)

    def leaf_copy(i, e):
        rel = BLOCKS_A[i][1]
        way = 1 if BLOCKS_A[i][0] > 0 else -1
        return remote(lsend.at[i, e], leaf.at[i % 2, rows_of(rel, e)], lsend_sem.at[i, e], leaf_sem.at[i % 2, rel, e], dev(way, rel))

    def sibling_copy(cls, e):
        return remote(ysend.at[cls, e], ybuf.at[cls, rows_of(1, e)], ysend_sem.at[cls, e], ybuf_sem.at[cls, e], dev(0, 1))

    def unit(x_ref, e, u, blocks, first):
        w_copy(0, u).wait()
        w_copy(1, u).wait()
        up_phase(x_ref, e, u, blocks)

        @pl.when(u + 2 < units)
        def _():
            w_copy(0, u + 2).start()
            w_copy(1, u + 2).start()

        w_copy(2, u).wait()
        down_phase(e, u, blocks, first)

        @pl.when(u + 2 < units)
        def _():
            w_copy(2, u + 2).start()

        for i, (a, rel) in enumerate(blocks):
            if first and i < LEAF:
                leaf_copy(i, e).start()
            elif rel == 1:
                sibling_copy(CLASS[a], e).start()

    def first_unit(e, carry):
        for b in range(len(BLOCKS_A)):
            xa_copy(e, b).wait()

        @pl.when(e + 2 < experts)
        def _():
            start_xa(e + 2)

        @pl.when(e >= experts - 2)
        def _():
            start_xb(0, e - (experts - 2))

        unit(xa.at[e], e, e, BLOCKS_A, True)
        return carry

    lax.fori_loop(0, experts, first_unit, 0)

    for a, cls in meta_to:
        meta_copy(a, cls).wait_recv()
    scr[...] = meta[...].T
    col = lax.broadcasted_iota(jnp.int32, (tokens, 2 * per_core), 1)
    order = lax.rem(col + k * per_core, 2 * per_core)

    def select(where, cls, a_chip):
        chip = lax.rem(z + a_chip * sigma + zn, zn)
        want = (order + chip * (2 * per_core)).astype(jnp.float32)
        weight = jnp.zeros((tokens, 2 * per_core), jnp.float32)
        for j in range(top_k):
            c = 2 * top_k * cls + j
            weight = jnp.where(scr[:, c:c + 1] == want, scr[:, c + top_k:c + top_k + 1], weight)
        for i in range(3):
            piece = weight.astype(jnp.bfloat16)
            sel[where, i * tokens:(i + 1) * tokens] = piece
            weight = weight - piece.astype(jnp.float32)

    def weigh(where, rows_ref, cols):
        rows = rows_ref[:, cols]
        p = jnp.dot(sel[where], rows, preferred_element_type=jnp.float32)
        return p[0:tokens] + p[tokens:2 * tokens] + p[2 * tokens:3 * tokens]

    def part_copy(src, to, c, a):
        return remote(src, part.at[to, c], psend_sem.at[to, c], part_sem.at[to, c], dev(a, 0))

    def wait_sibling(cls):
        for e in range(experts):
            sibling_copy(cls, e).wait_recv()

    def columns(c):
        return pl.ds(pl.multiple_of(c * width, width), width)

    for i, cls in enumerate((0, 1)):
        select(2 * i, cls, -1 if i == 0 else 1)
        select(2 * i + 1, cls, 0)
    for cls in (0, 1):
        wait_sibling(cls)
    for i in range(LEAF):
        for e in range(experts):
            leaf_copy(i, e).wait_recv()

    def second(c, carry):
        for i in range(2):
            head[i, c] = (weigh(2 * i, leaf.at[i], columns(c))
                          + weigh(2 * i + 1, ybuf.at[i], columns(c)))
            part_copy(head.at[i, c], i, c, 1 if i == 0 else -1).start()
        return carry

    lax.fori_loop(0, chunks, second, 0)

    def later_unit(p):
        def body(e, carry):
            for b in range(len(BLOCKS_B[p])):
                xb_copy(p, e, b).wait()
            if p == 0:
                @pl.when(e + 2 < experts)
                def _():
                    start_xb(0, e + 2)

                @pl.when(e >= experts - 2)
                def _():
                    start_xb(1, e - (experts - 2))
            else:
                @pl.when(e + 2 < experts)
                def _():
                    start_xb(1, e + 2)
            unit(xb.at[p, e], e, experts * (p + 1) + e, BLOCKS_B[p], False)
            return carry
        return body

    lax.fori_loop(0, experts, later_unit(0), 0)
    select(0, 2, 0)
    select(1, 3, 0)
    wait_sibling(2)
    wait_sibling(3)

    def third(c, carry):
        for i in range(2):
            mine = weigh(i, ybuf.at[2 + i], columns(c))
            way = 1 if i == 0 else -1
            part_copy(head.at[i, c], i, c, way).wait_recv()
            part[i, c] = part[i, c] + mine
            part_copy(part.at[i, c], 2 + i, c, way).start()
        return carry

    lax.fori_loop(0, chunks, third, 0)

    lax.fori_loop(0, experts, later_unit(1), 0)
    select(0, 4, 0)
    select(1, 5, 0)
    wait_sibling(4)
    wait_sibling(5)

    def fourth(c, carry):
        mine = weigh(0, ybuf.at[4], columns(c))
        part_copy(part.at[0, c], 2, c, 1).wait_recv()
        part[2, c] = part[2, c] + mine
        part_copy(part.at[2, c], 4, c, 1).start()
        return carry

    lax.fori_loop(0, chunks, fourth, 0)

    def last(c, carry):
        mine = weigh(1, ybuf.at[5], columns(c))
        part_copy(part.at[1, c], 3, c, -1).wait_recv()
        mine = mine + part[3, c]
        part_copy(part.at[2, c], 4, c, 1).wait_recv()
        out[:, columns(c)] = (mine + part[4, c]).astype(out.dtype)
        return carry

    lax.fori_loop(0, chunks, last, 0)

    for a, cls in meta_to:
        meta_copy(a, cls).wait_send()

    def sent_rows(e, carry):
        for i in range(LEAF):
            leaf_copy(i, e).wait_send()
        for cls in range(6):
            sibling_copy(cls, e).wait_send()
        return carry

    lax.fori_loop(0, experts, sent_rows, 0)

    def sent_parts(c, carry):
        part_copy(head.at[0, c], 0, c, 1).wait_send()
        part_copy(head.at[1, c], 1, c, -1).wait_send()
        part_copy(part.at[0, c], 2, c, 1).wait_send()
        part_copy(part.at[1, c], 3, c, -1).wait_send()
        part_copy(part.at[2, c], 4, c, 1).wait_send()
        return carry

    lax.fori_loop(0, chunks, sent_parts, 0)


def solution(mesh):
    zn = mesh.shape["ep"] // 2

    def local_step(dispatched, w_gate, w_up, w_down, fill_count, slot_index, expert_id, gate_weight):
        sources, experts, cap, dim = dispatched.shape
        ffn = w_gate.shape[2]
        tokens = slot_index.shape[0]
        bf16, f32 = jnp.bfloat16, jnp.float32
        width = TILE
        chunks = dim // width
        rows_a, rows_b = len(BLOCKS_A) * cap, len(BLOCKS_B[0]) * cap
        any_spec, vmem = pl.BlockSpec(memory_space=pl.ANY), pl.BlockSpec(memory_space=pltpu.VMEM)
        dma = pltpu.SemaphoreType.DMA
        return pl.pallas_call(
            functools.partial(kernel, zn),
            out_shape=jax.ShapeDtypeStruct((tokens, dim), bf16),
            in_specs=[any_spec] * 4 + [pl.BlockSpec(memory_space=pltpu.SMEM)] + [vmem] * 3,
            out_specs=vmem,
            scratch_shapes=[
                pltpu.VMEM((experts, rows_a, dim), bf16),
                pltpu.VMEM((2, experts, rows_b, dim), bf16),
                pltpu.VMEM((2, dim, ffn), bf16),
                pltpu.VMEM((2, dim, ffn), bf16),
                pltpu.VMEM((2, ffn, dim), bf16),
                pltpu.VMEM((rows_a, ffn), bf16),
                pltpu.VMEM((LEAF, experts, cap, dim), bf16),
                pltpu.VMEM((2, 2 * experts * cap, dim), bf16),
                pltpu.VMEM((6, experts, cap, dim), bf16),
                pltpu.VMEM((6, 2 * experts * cap, dim), bf16),
                pltpu.VMEM((2, chunks, tokens, width), f32),
                pltpu.VMEM((5, chunks, tokens, width), f32),
                pltpu.VMEM((128, tokens), f32),
                pltpu.VMEM((128, 128), f32),
                pltpu.VMEM((4, 3 * tokens, 2 * experts * cap), bf16),
                dma((experts, len(BLOCKS_A))),
                dma((2, experts, len(BLOCKS_B[0]))),
                dma((3, 2)),
                dma((LEAF, experts)),
                dma((2, 2, experts)),
                dma((6, experts)),
                dma((6, experts)),
                dma((5, chunks)),
                dma((5, chunks)),
                dma((5,)),
                dma((5,)),
            ],
            compiler_params=pltpu.CompilerParams(
                collective_id=0, has_side_effects=True, vmem_limit_bytes=67043328),
        )(dispatched, w_gate, w_up, w_down, fill_count, slot_index, expert_id, gate_weight)

    token_spec = P(("dp", "ep"))
    in_specs = (P("dp", "ep"), P("ep"), P("ep"), P("ep"), P("dp", "ep"), token_spec, token_spec, token_spec)
    return jax.shard_map(local_step, mesh=mesh, in_specs=in_specs, out_specs=token_spec, check_vma=False)
```

time: 282 us -> 108 us (0.38)
  waiting for transfers between devices: 188 us -> 0 us
  Pallas kernels: 0 us -> 101 us
  matrix products: 53.7 us -> 0 us
  local copies, waits for them, and re-layouts: 22 us -> 7.44 us
  starting transfers between devices: 9.73 us -> 0 us
  other arithmetic: 7.05 us -> 0 us
    all_to_all x1 -> x0, waiting for transfers between devices: 188 us -> none  [local_step(): returned = lax.all_to_all(result, 'ep', 1, 0, tiled=True)]
    pallas_call x0 -> x1, Pallas kernels: none -> 101 us  [local_step(): pl.pallas_call(functools.partial(kernel, zn), out_shape=jax.ShapeDtypeStr...]
    dot_general x3 -> x0, matrix products: 53.7 us -> none  [the longest x1 19.3 us: expert_rows(): jnp.einsum('secd,edf->escf', dispatched, w_gate, preferred_element_type=j...]
    gather x1 -> x0, local copies, waits for them, and re-layouts: 13.3 us -> none  [local_step(): picked = jnp.take(flat_rows, row_index, axis=0)]
    all_to_all x1 -> x0, starting transfers between devices: 9.73 us -> none  [local_step(): returned = lax.all_to_all(result, 'ep', 1, 0, tiled=True)]
    select_n x3 -> x0, local copies, waits for them, and re-layouts: 8.47 us -> none  [the longest x1 8.27 us: expert_rows(): return jnp.where(live_mask[..., None], result, 0)]
    unnamed x6 -> x5, local copies, waits for them, and re-layouts: 0.01 us -> 7.44 us
    reduce_sum x1 -> x0, other arithmetic: 6.27 us -> none  [local_step(): combined = jnp.sum(weight[:, :, None] * picked.astype(jnp.float32), axis=1)]
  transfers between devices with their start and end apart: 1 -> 0, of which waited for: 1 -> 0; matrix products, arithmetic and copies ran while one was open for 0% -> 0% of each run, Pallas kernels for 0% -> 0%
where the time goes in v1:
time: 108 us
  Pallas kernels  101 us (94%)
  local copies, waits for them, and re-layouts  7.44 us (7%)
    pallas_call x1, Pallas kernels, local_step(): pl.pallas_call(functools.partial(kernel, zn), out_shape=jax.ShapeDtypeStr...  101 us
    unnamed x5, local copies, waits for them, and re-layouts  7.44 us

profile of v1, /device:TPU:30, one launch (start us, length us, event | category | flops | bytes accessed | tf_op | source)
XLA Modules:
  0.0 108.1 jit_solution(3549808084332419882)
XLA Ops:
  0.0 1.3 %copy.9.fill = s32[16,4]{1,0:T(8,128)} copy(s32[16,4]{0,1:T(4,128)} %param.12) | data formatting | bytes 512 | tf_op args[4]
  1.3 1.4 %copy.10.slot = s32[128,8]{1,0:T(8,128)} copy(s32[128,8]{0,1:T(8,128)} %param.13) | data formatting | bytes 8192 | tf_op args[5]
  2.7 1.4 %copy.11.eid = s32[128,8]{1,0:T(8,128)} copy(s32[128,8]{0,1:T(8,128)} %param.14) | data formatting | bytes 8192 | tf_op args[6]
  4.2 1.4 %copy.12.gw = f32[128,8]{1,0:T(8,128)} copy(f32[128,8]{0,1:T(8,128)} %param.15) | data formatting | bytes 8192 | tf_op args[7]
  5.6 100.7 %shard_map.82 = bf16[128,2048]{1,0:T(8,128)(2,1)} custom-call(bf16[16,4,32,2048]{3,2,1,0:T(8,128)(2,1)} %disp.1, bf16[4,2048,1024]{2,1,0:T(8,128)(2,1)} %wg.1, bf16[4,2048,1024]{2,1,0:T(8,128)(2,1)} %wu.1, bf16[4,1024,2048]{2,1,0:T(8,128)(2,1)} %wd.1, s32[16,4]{1,0:T(8,128)} %copy.9.fill, s32[128,8]{1,0:T(8,128)} %copy.10.slot, s32[128,8]{1,0:T(8,128)} %copy.11.eid, ...), custom_call_target="tpu_custom_call" | custom-call | tf_op jit(solution)/shard_map/pallas_call | solution.py:323
  106.2 1.9 %copy.14 = bf16[128,2048]{1,0:T(8,128)(2,1)} copy(bf16[128,2048]{1,0:T(8,128)(2,1)} %shard_map.82) | data formatting | bytes 1048576

commit v2 on v0

v2 whole, which is shorter than its diff:
```python
import functools

import jax
import jax.numpy as jnp
from jax import lax
from jax.experimental import pallas as pl
from jax.experimental.pallas import tpu as pltpu
from jax.sharding import PartitionSpec as P

MESH = pl.DeviceIdType.MESH
BLOCKS_L = ((4, 0), (-3, 0), (4, 1), (-3, 1))
BLOCKS_R = ((3, 0), (-2, 0), (3, 1), (-2, 1))
BLOCKS_A = (BLOCKS_L, BLOCKS_R)
BLOCKS_B = (((2, 0), (-1, 0), (2, 1), (-1, 1)), ((1, 0), (0, 0), (1, 1), (0, 1)))
CLASS = {3: 0, -2: 1, 2: 2, -1: 3, 1: 4, 0: 5}
TILE = 512


def kernel(zn, disp, wg, wu, wd, fill_hbm, slot_hbm, eid_hbm, gw_hbm, out,
           xa, xb, wgb, wub, wdb, hid, lsend, leaf, ysend, ybuf, head, part, meta, scr, sel, outv, fill, slot, eid, gw,
           x_sem, gu_sem, d_sem, small_sem, leaf_sem, ybuf_sem, part_sem, meta_sem, send_sem, out_sem):
    me = lax.axis_index("ep")
    z, k = me // 2, lax.rem(me, 2)
    sigma = 1 - 2 * k
    experts, cap, dim = disp.shape[1:]
    ffn = wg.shape[2]
    top_k, tokens = slot.shape
    per_core = experts * cap
    chunks, _, width = part.shape[1:]
    ups = ffn // width
    rows = len(BLOCKS_L) * cap
    lsend_sem, ysend_sem, head_sem, psend_sem, msend_sem = (send_sem.at[i] for i in range(5))

    def dev(a, rel):
        chip = lax.rem(z + a * sigma + zn, zn) if rel == 0 else lax.rem(z - a * sigma + zn, zn)
        return 2 * chip + (k if rel == 0 else 1 - k)

    def remote(src, dst, send, recv, target):
        return pltpu.make_async_remote_copy(src_ref=src, dst_ref=dst, send_sem=send, recv_sem=recv,
                                            device_id={"ep": target}, device_id_type=MESH)

    def rows_of(core, e):
        return pl.ds(pl.multiple_of(core * per_core + e * cap, cap), cap)

    def rows_meta(cls):
        return pl.ds(2 * top_k * cls, 2 * top_k)

    def columns(c):
        return pl.ds(pl.multiple_of(c * width, width), width)

    def x_copy(h, e, b):
        x, blocks = (xa, BLOCKS_A[h]) if h < 2 else (xb, BLOCKS_B[h - 2])
        return pltpu.make_async_copy(disp.at[dev(*blocks[b]), e], x.at[h % 2, e, pl.ds(b * cap, cap)], x_sem.at[h, e])

    def gu_copy(which, e, n):
        src, dst = ((wg, wgb), (wu, wub))[which]
        return pltpu.make_async_copy(src.at[e, :, columns(n)], dst.at[lax.rem(e, 2), :, columns(n)],
                                     gu_sem.at[which, lax.rem(e, 2), n])

    def d_copy(e, n):
        return pltpu.make_async_copy(wd.at[e, :, columns(n)], wdb.at[lax.rem(e, 2), :, columns(n)], d_sem.at[lax.rem(e, 2), n])

    def start_gu(e):
        for n in range(ups):
            for which in range(2):
                gu_copy(which, e, n).start()

    def start_d(e):
        for n in range(chunks):
            d_copy(e, n).start()

    def start_x(h, e):
        for b in range(len(BLOCKS_L)):
            x_copy(h, e, b).start()

    def arrived(ref, sem):
        pltpu.make_async_copy(ref, ref, sem).wait()

    def wait_x(h, e):
        arrived((xa if h < 2 else xb).at[h % 2, e], x_sem.at[h, e])

    small = [pltpu.make_async_copy(src, dst, small_sem.at[i]) for i, (src, dst) in enumerate(
        ((fill_hbm, fill), (slot_hbm, slot), (eid_hbm, eid), (gw_hbm, gw)))]
    start_x(0, 0)
    start_gu(0)
    for copy in small:
        copy.start()
    start_d(0)
    for copy in small:
        copy.wait()

    flat = jnp.where(slot[...] >= 0, eid[...] * cap + slot[...], -1)
    meta[...] = jnp.zeros_like(meta)
    meta[2 * top_k * CLASS[0]:2 * top_k * CLASS[0] + top_k] = flat.astype(jnp.float32)
    meta[2 * top_k * CLASS[0] + top_k:2 * top_k * (CLASS[0] + 1)] = gw[...]

    barrier = pltpu.get_barrier_semaphore()
    partners = [(0, 1), (1, 0), (-1, 0), (1, 1), (-1, 1), (2, 0), (-2, 0), (3, 0), (-3, 0)]
    for a, rel in partners:
        pl.semaphore_signal(barrier, inc=1, device_id={"ep": dev(a, rel)}, device_id_type=MESH)

    def up_phase(x_ref, e, blocks, wait):
        s = lax.rem(e, 2)
        row = lax.broadcasted_iota(jnp.int32, (cap, width), 0)

        def tile(n, carry):
            cols = columns(n)
            if wait:
                for which in range(2):
                    gu_copy(which, e, n).wait()
            x = x_ref[...]
            a = jnp.dot(x, wgb[s, :, cols], preferred_element_type=jnp.float32)
            b = jnp.dot(x, wub[s, :, cols], preferred_element_type=jnp.float32)
            h = jax.nn.silu(a) * b
            for i, block in enumerate(blocks):
                live = row < fill[e, dev(*block)]
                hid[i * cap:(i + 1) * cap, cols] = jnp.where(live, h[i * cap:(i + 1) * cap], 0.0).astype(jnp.bfloat16)
            return carry

        lax.fori_loop(0, ups, tile, 0)

    def leaf_copy(i, e, c):
        a, rel = BLOCKS_L[i]
        return remote(lsend.at[i, e, c], leaf.at[i % 2, c, rows_of(rel, e)], lsend_sem,
                      leaf_sem.at[i % 2, c], dev(1 if a > 0 else -1, rel))

    def sibling_copy(cls, e):
        return remote(ysend.at[cls, e], ybuf.at[cls, :, rows_of(1, e)], ysend_sem, ybuf_sem.at[cls], dev(0, 1))

    def down_phase(e, blocks, wait):
        s = lax.rem(e, 2)
        leaves = blocks is BLOCKS_L

        def tile(n, carry):
            if wait:
                d_copy(e, n).wait()
            y = jnp.dot(hid[...], wdb[s, :, columns(n)], preferred_element_type=jnp.float32).astype(jnp.bfloat16)
            for i, (a, rel) in enumerate(blocks):
                block = y[i * cap:(i + 1) * cap]
                if leaves:
                    lsend[i, e, n] = block
                elif rel == 0:
                    ybuf[CLASS[a], n, rows_of(0, e)] = block
                else:
                    ysend[CLASS[a], e, n] = block
            if leaves:
                for i in range(len(blocks)):
                    leaf_copy(i, e, n).start()
            return carry

        lax.fori_loop(0, chunks, tile, 0)
        if not leaves:
            for a, rel in blocks:
                if rel == 1:
                    sibling_copy(CLASS[a], e).start()

    meta_to = [(-3, 0), (2, 1), (-2, 2), (1, 3), (-1, 4)]

    def meta_copy(a, cls):
        return remote(meta.at[rows_meta(CLASS[0])], meta.at[rows_meta(cls)], msend_sem, meta_sem.at[0], dev(a, 0))

    def leaf_unit(e, carry):
        wait_x(0, e)
        up_phase(xa.at[0, e], e, BLOCKS_L, True)
        down_phase(e, BLOCKS_L, True)
        return carry

    def rest_unit(e, carry, load):
        wait_x(1, e)
        up_phase(xa.at[1, e], e, BLOCKS_R, False)
        if load:
            start_gu(e + 2)
        down_phase(e, BLOCKS_R, False)
        if load:
            start_d(e + 2)
        return carry

    wait_x(0, 0)
    up_phase(xa.at[0, 0], 0, BLOCKS_L, True)
    start_x(0, 1)
    start_gu(1)
    start_d(1)
    for e in range(2):
        start_x(1, e)
    pl.semaphore_wait(barrier, len(partners))
    for a, cls in meta_to:
        meta_copy(a, cls).start()
    down_phase(0, BLOCKS_L, True)
    leaf_unit(1, 0)
    for e in range(2, experts):
        start_x(0, e)
        start_x(1, e)
    lax.fori_loop(0, 2, functools.partial(rest_unit, load=True), 0)
    for e in range(experts):
        start_x(2, e)
    lax.fori_loop(2, experts, leaf_unit, 0)

    arrived(meta.at[pl.ds(0, 2 * top_k * len(meta_to))], meta_sem.at[0])
    scr[...] = meta[...].T
    col = lax.broadcasted_iota(jnp.int32, (tokens, 2 * per_core), 1)
    order = lax.rem(col + k * per_core, 2 * per_core)

    def select(where, cls, a_chip):
        chip = lax.rem(z + a_chip * sigma + zn, zn)
        want = (order + chip * (2 * per_core)).astype(jnp.float32)
        weight = jnp.zeros((tokens, 2 * per_core), jnp.float32)
        for j in range(top_k):
            c = 2 * top_k * cls + j
            weight = jnp.where(scr[:, c:c + 1] == want, scr[:, c + top_k:c + top_k + 1], weight)
        for i in range(3):
            piece = weight.astype(jnp.bfloat16)
            sel[where, i * tokens:(i + 1) * tokens] = piece
            weight = weight - piece.astype(jnp.float32)

    def weigh(where, rows_ref):
        p = jnp.dot(sel[where], rows_ref[...], preferred_element_type=jnp.float32)
        return p[0:tokens] + p[tokens:2 * tokens] + p[2 * tokens:3 * tokens]

    def part_copy(src, to, c, a):
        return remote(src, part.at[to, c], head_sem if to < 2 else psend_sem, part_sem.at[to, c], dev(a, 0))

    def wait_part(to, c):
        arrived(part.at[to, c], part_sem.at[to, c])

    def wait_sibling(cls):
        arrived(ybuf.at[cls, :, pl.ds(per_core, per_core)], ybuf_sem.at[cls])

    for cls in (0, 1):
        select(cls, cls, 0)
        select(6 + cls, cls, -1 if cls == 0 else 1)
    lax.fori_loop(2, experts, functools.partial(rest_unit, load=False), 0)

    for cls in (0, 1):
        wait_sibling(cls)

    def second(c, carry):
        for i in range(2):
            mine = weigh(i, ybuf.at[i, c])
            arrived(leaf.at[i, c], leaf_sem.at[i, c])
            head[i, c] = mine + weigh(6 + i, leaf.at[i, c])
            part_copy(head.at[i, c], i, c, 1 if i == 0 else -1).start()
        return carry

    lax.fori_loop(0, chunks, second, 0)

    def later_unit(p, half):
        def body(q, carry):
            e = q + 2 * ((p + half + 1) % 2)
            wait_x(2 + p, e)
            up_phase(xb.at[p, e], e, BLOCKS_B[p], half == 1)
            if half == 0:
                start_gu(lax.rem(e + 2, experts))
            down_phase(e, BLOCKS_B[p], half == 1)
            if half == 0:
                start_d(lax.rem(e + 2, experts))
            return carry
        return body

    def later_pass(p):
        for half in range(2):
            lax.fori_loop(0, 2, later_unit(p, half), 0)

    for cls in range(2, 6):
        select(cls, cls, 0)
    for e in range(experts):
        start_x(3, e)
    later_pass(0)
    wait_sibling(2)
    wait_sibling(3)

    def third(c, carry):
        for i in range(2):
            mine = weigh(2 + i, ybuf.at[2 + i, c])
            way = 1 if i == 0 else -1
            wait_part(i, c)
            part[i, c] = part[i, c] + mine
            part_copy(part.at[i, c], 2 + i, c, way).start()
        return carry

    lax.fori_loop(0, chunks, third, 0)

    later_pass(1)
    wait_sibling(4)
    wait_sibling(5)

    def fourth(c, carry):
        mine = weigh(4, ybuf.at[4, c])
        wait_part(2, c)
        part[2, c] = part[2, c] + mine
        part_copy(part.at[2, c], 4, c, 1).start()
        return carry

    lax.fori_loop(0, chunks, fourth, 0)

    def out_copy(c):
        return pltpu.make_async_copy(outv.at[c], out.at[:, columns(c)], out_sem.at[0])

    def last(c, carry):
        mine = weigh(5, ybuf.at[5, c])
        wait_part(3, c)
        mine = mine + part[3, c]
        wait_part(4, c)
        outv[c] = (mine + part[4, c]).astype(out.dtype)
        out_copy(c).start()
        return carry

    lax.fori_loop(0, chunks, last, 0)

    arrived(outv, out_sem.at[0])
    arrived(meta.at[pl.ds(0, 2 * top_k * len(meta_to))], msend_sem)
    arrived(lsend, lsend_sem)
    arrived(ysend, ysend_sem)
    arrived(head, head_sem)
    arrived(part.at[pl.ds(0, 3)], psend_sem)


def solution(mesh):
    zn = mesh.shape["ep"] // 2

    def local_step(dispatched, w_gate, w_up, w_down, fill_count, slot_index, expert_id, gate_weight):
        sources, experts, cap, dim = dispatched.shape
        ffn = w_gate.shape[2]
        tokens = slot_index.shape[0]
        bf16, f32 = jnp.bfloat16, jnp.float32
        width = TILE
        chunks = dim // width
        blocks = len(BLOCKS_L)
        rows = blocks * cap
        any_spec = pl.BlockSpec(memory_space=pl.ANY)
        dma = pltpu.SemaphoreType.DMA
        return pl.pallas_call(
            functools.partial(kernel, zn),
            out_shape=jax.ShapeDtypeStruct((tokens, dim), bf16),
            in_specs=[any_spec] * 8,
            out_specs=any_spec,
            scratch_shapes=[
                pltpu.VMEM((2, experts, rows, dim), bf16),
                pltpu.VMEM((2, experts, rows, dim), bf16),
                pltpu.VMEM((2, dim, ffn), bf16),
                pltpu.VMEM((2, dim, ffn), bf16),
                pltpu.VMEM((2, ffn, dim), bf16),
                pltpu.VMEM((rows, ffn), bf16),
                pltpu.VMEM((blocks, experts, chunks, cap, width), bf16),
                pltpu.VMEM((2, chunks, 2 * experts * cap, width), bf16),
                pltpu.VMEM((6, experts, chunks, cap, width), bf16),
                pltpu.VMEM((6, chunks, 2 * experts * cap, width), bf16),
                pltpu.VMEM((2, chunks, tokens, width), f32),
                pltpu.VMEM((5, chunks, tokens, width), f32),
                pltpu.VMEM((128, tokens), f32),
                pltpu.VMEM((128, 128), f32),
                pltpu.VMEM((8, 3 * tokens, 2 * experts * cap), bf16),
                pltpu.VMEM((chunks, tokens, width), bf16),
                pltpu.SMEM((experts, sources), jnp.int32),
                pltpu.VMEM(slot_index.shape[::-1], jnp.int32),
                pltpu.VMEM(expert_id.shape[::-1], jnp.int32),
                pltpu.VMEM(gate_weight.shape[::-1], f32),
                dma((4, experts)),
                dma((2, 2, ffn // width)),
                dma((2, chunks)),
                dma((4,)),
                dma((2, chunks)),
                dma((6,)),
                dma((5, chunks)),
                dma((1,)),
                dma((5,)),
                dma((1,)),
            ],
            compiler_params=pltpu.CompilerParams(
                collective_id=0, has_side_effects=True, vmem_limit_bytes=67043328),
        )(dispatched, w_gate, w_up, w_down, fill_count.T, slot_index.T, expert_id.T, gate_weight.T)

    token_spec = P(("dp", "ep"))
    in_specs = (P("dp", "ep"), P("ep"), P("ep"), P("ep"), P("dp", "ep"), token_spec, token_spec, token_spec)
    return jax.shard_map(local_step, mesh=mesh, in_specs=in_specs, out_specs=token_spec, check_vma=False)
```

time: 282 us -> 101 us (0.36)
  waiting for transfers between devices: 188 us -> 0 us
  Pallas kernels: 0 us -> 99.4 us
  matrix products: 53.7 us -> 0 us
  local copies, waits for them, and re-layouts: 22 us -> 1.88 us
  starting transfers between devices: 9.73 us -> 0 us
  other arithmetic: 7.05 us -> 0 us
    all_to_all x1 -> x0, waiting for transfers between devices: 188 us -> none  [local_step(): returned = lax.all_to_all(result, 'ep', 1, 0, tiled=True)]
    pallas_call x0 -> x1, Pallas kernels: none -> 99.4 us  [local_step(): pl.pallas_call(functools.partial(kernel, zn), out_shape=jax.ShapeDtypeStr...]
    dot_general x3 -> x0, matrix products: 53.7 us -> none  [the longest x1 19.3 us: expert_rows(): jnp.einsum('secd,edf->escf', dispatched, w_gate, preferred_element_type=j...]
    gather x1 -> x0, local copies, waits for them, and re-layouts: 13.3 us -> none  [local_step(): picked = jnp.take(flat_rows, row_index, axis=0)]
    all_to_all x1 -> x0, starting transfers between devices: 9.73 us -> none  [local_step(): returned = lax.all_to_all(result, 'ep', 1, 0, tiled=True)]
    select_n x3 -> x0, local copies, waits for them, and re-layouts: 8.47 us -> none  [the longest x1 8.27 us: expert_rows(): return jnp.where(live_mask[..., None], result, 0)]
    reduce_sum x1 -> x0, other arithmetic: 6.27 us -> none  [local_step(): combined = jnp.sum(weight[:, :, None] * picked.astype(jnp.float32), axis=1)]
  transfers between devices with their start and end apart: 1 -> 0, of which waited for: 1 -> 0; matrix products, arithmetic and copies ran while one was open for 0% -> 0% of each run, Pallas kernels for 0% -> 0%
where the time goes in v2:
time: 101 us
  Pallas kernels  99.4 us (98%)
  local copies, waits for them, and re-layouts  1.88 us (2%)
    pallas_call x1, Pallas kernels, local_step(): pl.pallas_call(functools.partial(kernel, zn), out_shape=jax.ShapeDtypeStr...  99.4 us

profile of v2, /device:TPU:30, one launch (start us, length us, event | category | flops | bytes accessed | tf_op | source)
XLA Modules:
  0.0 101.3 jit_solution(3862017373448759113)
XLA Ops:
  0.0 99.4 %shard_map.82 = bf16[128,2048]{1,0:T(8,128)(2,1)} custom-call(bf16[16,4,32,2048]{3,2,1,0:T(8,128)(2,1)} %disp.1, bf16[4,2048,1024]{2,1,0:T(8,128)(2,1)} %wg.1, bf16[4,2048,1024]{2,1,0:T(8,128)(2,1)} %wu.1, bf16[4,1024,2048]{2,1,0:T(8,128)(2,1)} %wd.1, s32[4,16]{1,0:T(4,128)} %bitcast.7, s32[8,128]{1,0:T(8,128)} %bitcast.4, s32[8,128]{1,0:T(8,128)} %bitcast.5, ...), custom_call_target="tpu_custom_call" | custom-call | tf_op jit(solution)/shard_map/pallas_call | solution.py:331
  99.4 1.9 %copy.10 = bf16[128,2048]{1,0:T(8,128)(2,1)} copy(bf16[128,2048]{1,0:T(8,128)(2,1)} %shard_map.82) | data formatting | bytes 1048576

commit v3 on v2

--- a/solution.py
+++ b/solution.py
@@ -14,6 +14,7 @@
 BLOCKS_B = (((2, 0), (-1, 0), (2, 1), (-1, 1)), ((1, 0), (0, 0), (1, 1), (0, 1)))
 CLASS = {3: 0, -2: 1, 2: 2, -1: 3, 1: 4, 0: 5}
 TILE = 512
+UP_TILE = 512
 
 
 def kernel(zn, disp, wg, wu, wd, fill_hbm, slot_hbm, eid_hbm, gw_hbm, out,
@@ -27,7 +28,7 @@
     top_k, tokens = slot.shape
     per_core = experts * cap
     chunks, _, width = part.shape[1:]
-    ups = ffn // width
+    ups = ffn // UP_TILE
     rows = len(BLOCKS_L) * cap
     lsend_sem, ysend_sem, head_sem, psend_sem, msend_sem = (send_sem.at[i] for i in range(5))
 
@@ -45,16 +46,16 @@
     def rows_meta(cls):
         return pl.ds(2 * top_k * cls, 2 * top_k)
 
-    def columns(c):
-        return pl.ds(pl.multiple_of(c * width, width), width)
+    def columns(c, wide=width):
+        return pl.ds(pl.multiple_of(c * wide, wide), wide)
 
     def x_copy(h, e, b):
         x, blocks = (xa, BLOCKS_A[h]) if h < 2 else (xb, BLOCKS_B[h - 2])
-        return pltpu.make_async_copy(disp.at[dev(*blocks[b]), e], x.at[h % 2, e, pl.ds(b * cap, cap)], x_sem.at[h, e])
+        return pltpu.make_async_copy(disp.at[dev(*blocks[b]), e], x.at[h % 2, e, pl.ds(b * cap, cap)], x_sem.at[h, e if h < 2 else 0])
 
     def gu_copy(which, e, n):
         src, dst = ((wg, wgb), (wu, wub))[which]
-        return pltpu.make_async_copy(src.at[e, :, columns(n)], dst.at[lax.rem(e, 2), :, columns(n)],
+        return pltpu.make_async_copy(src.at[e, :, columns(n, UP_TILE)], dst.at[lax.rem(e, 2), :, columns(n, UP_TILE)],
                                      gu_sem.at[which, lax.rem(e, 2), n])
 
     def d_copy(e, n):
@@ -77,7 +78,7 @@
         pltpu.make_async_copy(ref, ref, sem).wait()
 
     def wait_x(h, e):
-        arrived((xa if h < 2 else xb).at[h % 2, e], x_sem.at[h, e])
+        arrived(xa.at[h, e], x_sem.at[h, e])
 
     small = [pltpu.make_async_copy(src, dst, small_sem.at[i]) for i, (src, dst) in enumerate(
         ((fill_hbm, fill), (slot_hbm, slot), (eid_hbm, eid), (gw_hbm, gw)))]
@@ -101,10 +102,10 @@
 
     def up_phase(x_ref, e, blocks, wait):
         s = lax.rem(e, 2)
-        row = lax.broadcasted_iota(jnp.int32, (cap, width), 0)
+        row = lax.broadcasted_iota(jnp.int32, (cap, UP_TILE), 0)
 
         def tile(n, carry):
-            cols = columns(n)
+            cols = columns(n, UP_TILE)
             if wait:
                 for which in range(2):
                     gu_copy(which, e, n).wait()
@@ -117,7 +118,7 @@
                 hid[i * cap:(i + 1) * cap, cols] = jnp.where(live, h[i * cap:(i + 1) * cap], 0.0).astype(jnp.bfloat16)
             return carry
 
-        lax.fori_loop(0, ups, tile, 0)
+        lax.fori_loop(0, ups, tile, 0, unroll=True)
 
     def leaf_copy(i, e, c):
         a, rel = BLOCKS_L[i]
@@ -148,7 +149,7 @@
                     leaf_copy(i, e, n).start()
             return carry
 
-        lax.fori_loop(0, chunks, tile, 0)
+        lax.fori_loop(0, chunks, tile, 0, unroll=True)
         if not leaves:
             for a, rel in blocks:
                 if rel == 1:
@@ -193,7 +194,6 @@
     lax.fori_loop(0, 2, functools.partial(rest_unit, load=True), 0)
     for e in range(experts):
         start_x(2, e)
-    lax.fori_loop(2, experts, leaf_unit, 0)
 
     arrived(meta.at[pl.ds(0, 2 * top_k * len(meta_to))], meta_sem.at[0])
     scr[...] = meta[...].T
@@ -212,6 +212,13 @@
             sel[where, i * tokens:(i + 1) * tokens] = piece
             weight = weight - piece.astype(jnp.float32)
 
+    for cls in (0, 1):
+        select(cls, cls, 0)
+        select(6 + cls, cls, -1 if cls == 0 else 1)
+
+    lax.fori_loop(2, experts, leaf_unit, 0)
+
+
     def weigh(where, rows_ref):
         p = jnp.dot(sel[where], rows_ref[...], preferred_element_type=jnp.float32)
         return p[0:tokens] + p[tokens:2 * tokens] + p[2 * tokens:3 * tokens]
@@ -225,9 +232,6 @@
     def wait_sibling(cls):
         arrived(ybuf.at[cls, :, pl.ds(per_core, per_core)], ybuf_sem.at[cls])
 
-    for cls in (0, 1):
-        select(cls, cls, 0)
-        select(6 + cls, cls, -1 if cls == 0 else 1)
     lax.fori_loop(2, experts, functools.partial(rest_unit, load=False), 0)
 
     for cls in (0, 1):
@@ -246,7 +250,6 @@
     def later_unit(p, half):
         def body(q, carry):
             e = q + 2 * ((p + half + 1) % 2)
-            wait_x(2 + p, e)
             up_phase(xb.at[p, e], e, BLOCKS_B[p], half == 1)
             if half == 0:
                 start_gu(lax.rem(e + 2, experts))
@@ -257,6 +260,7 @@
         return body
 
     def later_pass(p):
+        arrived(xb.at[p], x_sem.at[2 + p, 0])
         for half in range(2):
             lax.fori_loop(0, 2, later_unit(p, half), 0)
 
@@ -355,7 +359,7 @@
                 pltpu.VMEM(expert_id.shape[::-1], jnp.int32),
                 pltpu.VMEM(gate_weight.shape[::-1], f32),
                 dma((4, experts)),
-                dma((2, 2, ffn // width)),
+                dma((2, 2, ffn // UP_TILE)),
                 dma((2, chunks)),
                 dma((4,)),
                 dma((2, chunks)),

time: 101 us -> 98.9 us (0.979)
  Pallas kernels: 99.4 us -> 96.9 us
    pallas_call x1, Pallas kernels: 99.4 us -> 96.9 us  [local_step(): pl.pallas_call(functools.partial(kernel, zn), out_shape=jax.ShapeDtypeStr...]
where the time goes in v3:
time: 98.9 us; the launch traced here: 98.8 us
  Pallas kernels  96.9 us (98%)
  local copies, waits for them, and re-layouts  1.88 us (2%)
    pallas_call x1, Pallas kernels, local_step(): pl.pallas_call(functools.partial(kernel, zn), out_shape=jax.ShapeDtypeStr...  96.9 us

profile of v3, /device:TPU:30, one launch (start us, length us, event | category | flops | bytes accessed | tf_op | source)
XLA Modules:
  0.0 98.8 jit_solution(3814927047242920089)
XLA Ops:
  0.0 96.9 %shard_map.82 = bf16[128,2048]{1,0:T(8,128)(2,1)} custom-call(bf16[16,4,32,2048]{3,2,1,0:T(8,128)(2,1)} %disp.1, bf16[4,2048,1024]{2,1,0:T(8,128)(2,1)} %wg.1, bf16[4,2048,1024]{2,1,0:T(8,128)(2,1)} %wu.1, bf16[4,1024,2048]{2,1,0:T(8,128)(2,1)} %wd.1, s32[4,16]{1,0:T(4,128)} %bitcast.7, s32[8,128]{1,0:T(8,128)} %bitcast.4, s32[8,128]{1,0:T(8,128)} %bitcast.5, ...), custom_call_target="tpu_custom_call" | custom-call | tf_op jit(solution)/shard_map/pallas_call | solution.py:335
  96.9 1.9 %copy.10 = bf16[128,2048]{1,0:T(8,128)(2,1)} copy(bf16[128,2048]{1,0:T(8,128)(2,1)} %shard_map.82) | data formatting | bytes 1048576

commit v4 on v3

--- a/solution.py
+++ b/solution.py
@@ -47,6 +47,8 @@
         return pl.ds(2 * top_k * cls, 2 * top_k)
 
     def columns(c, wide=width):
+        if isinstance(c, int):
+            return pl.ds(c * wide, wide)
         return pl.ds(pl.multiple_of(c * wide, wide), wide)
 
     def x_copy(h, e, b):
@@ -61,8 +63,8 @@
     def d_copy(e, n):
         return pltpu.make_async_copy(wd.at[e, :, columns(n)], wdb.at[lax.rem(e, 2), :, columns(n)], d_sem.at[lax.rem(e, 2), n])
 
-    def start_gu(e):
-        for n in range(ups):
+    def start_gu(e, tiles=None):
+        for n in range(ups) if tiles is None else tiles:
             for which in range(2):
                 gu_copy(which, e, n).start()
 
@@ -83,12 +85,12 @@
     small = [pltpu.make_async_copy(src, dst, small_sem.at[i]) for i, (src, dst) in enumerate(
         ((fill_hbm, fill), (slot_hbm, slot), (eid_hbm, eid), (gw_hbm, gw)))]
     start_x(0, 0)
-    start_gu(0)
+    start_gu(0, range(1))
     for copy in small:
         copy.start()
-    start_d(0)
     for copy in small:
         copy.wait()
+    start_gu(0, range(1, ups))
 
     flat = jnp.where(slot[...] >= 0, eid[...] * cap + slot[...], -1)
     meta[...] = jnp.zeros_like(meta)
@@ -100,15 +102,17 @@
     for a, rel in partners:
         pl.semaphore_signal(barrier, inc=1, device_id={"ep": dev(a, rel)}, device_id_type=MESH)
 
-    def up_phase(x_ref, e, blocks, wait):
+    def up_phase(x_ref, e, blocks, wait, after=None):
         s = lax.rem(e, 2)
         row = lax.broadcasted_iota(jnp.int32, (cap, UP_TILE), 0)
 
-        def tile(n, carry):
+        for n in range(ups):
             cols = columns(n, UP_TILE)
             if wait:
                 for which in range(2):
                     gu_copy(which, e, n).wait()
+            if after is not None and n == 0:
+                after()
             x = x_ref[...]
             a = jnp.dot(x, wgb[s, :, cols], preferred_element_type=jnp.float32)
             b = jnp.dot(x, wub[s, :, cols], preferred_element_type=jnp.float32)
@@ -116,9 +120,6 @@
             for i, block in enumerate(blocks):
                 live = row < fill[e, dev(*block)]
                 hid[i * cap:(i + 1) * cap, cols] = jnp.where(live, h[i * cap:(i + 1) * cap], 0.0).astype(jnp.bfloat16)
-            return carry
-
-        lax.fori_loop(0, ups, tile, 0, unroll=True)
 
     def leaf_copy(i, e, c):
         a, rel = BLOCKS_L[i]
@@ -128,13 +129,15 @@
     def sibling_copy(cls, e):
         return remote(ysend.at[cls, e], ybuf.at[cls, :, rows_of(1, e)], ysend_sem, ybuf_sem.at[cls], dev(0, 1))
 
-    def down_phase(e, blocks, wait):
+    def down_phase(e, blocks, wait, after=None):
         s = lax.rem(e, 2)
         leaves = blocks is BLOCKS_L
 
-        def tile(n, carry):
+        for n in range(chunks):
             if wait:
                 d_copy(e, n).wait()
+            if after is not None and n == 0:
+                after()
             y = jnp.dot(hid[...], wdb[s, :, columns(n)], preferred_element_type=jnp.float32).astype(jnp.bfloat16)
             for i, (a, rel) in enumerate(blocks):
                 block = y[i * cap:(i + 1) * cap]
@@ -147,9 +150,6 @@
             if leaves:
                 for i in range(len(blocks)):
                     leaf_copy(i, e, n).start()
-            return carry
-
-        lax.fori_loop(0, chunks, tile, 0, unroll=True)
         if not leaves:
             for a, rel in blocks:
                 if rel == 1:
@@ -160,40 +160,38 @@
     def meta_copy(a, cls):
         return remote(meta.at[rows_meta(CLASS[0])], meta.at[rows_meta(cls)], msend_sem, meta_sem.at[0], dev(a, 0))
 
-    def leaf_unit(e, carry):
+    def load_next(e):
+        start_x(0, e)
+        start_gu(e)
+        start_d(e)
+        start_x(1, e)
+
+    def rest_unit(e):
+        wait_x(1, e)
+        up_phase(xa.at[1, e], e, BLOCKS_R, False)
+        down_phase(e, BLOCKS_R, False)
+
+    def early_unit(e, carry):
+        def following():
+            @pl.when(e + 1 < experts)
+            def _():
+                load_next(e + 1)
+
         wait_x(0, e)
         up_phase(xa.at[0, e], e, BLOCKS_L, True)
-        down_phase(e, BLOCKS_L, True)
-        return carry
-
-    def rest_unit(e, carry, load):
-        wait_x(1, e)
-        up_phase(xa.at[1, e], e, BLOCKS_R, False)
-        if load:
-            start_gu(e + 2)
-        down_phase(e, BLOCKS_R, False)
-        if load:
-            start_d(e + 2)
+        down_phase(e, BLOCKS_L, True, following)
+        rest_unit(e)
         return carry
 
     wait_x(0, 0)
-    up_phase(xa.at[0, 0], 0, BLOCKS_L, True)
-    start_x(0, 1)
-    start_gu(1)
-    start_d(1)
-    for e in range(2):
-        start_x(1, e)
+    up_phase(xa.at[0, 0], 0, BLOCKS_L, True, lambda: start_d(0))
     pl.semaphore_wait(barrier, len(partners))
     for a, cls in meta_to:
         meta_copy(a, cls).start()
-    down_phase(0, BLOCKS_L, True)
-    leaf_unit(1, 0)
-    for e in range(2, experts):
-        start_x(0, e)
-        start_x(1, e)
-    lax.fori_loop(0, 2, functools.partial(rest_unit, load=True), 0)
-    for e in range(experts):
-        start_x(2, e)
+    start_x(1, 0)
+    down_phase(0, BLOCKS_L, True, lambda: load_next(1))
+    rest_unit(0)
+    lax.fori_loop(1, 2, early_unit, 0)
 
     arrived(meta.at[pl.ds(0, 2 * top_k * len(meta_to))], meta_sem.at[0])
     scr[...] = meta[...].T
@@ -216,7 +214,9 @@
         select(cls, cls, 0)
         select(6 + cls, cls, -1 if cls == 0 else 1)
 
-    lax.fori_loop(2, experts, leaf_unit, 0)
+    lax.fori_loop(2, experts, early_unit, 0)
+    for e in range(experts):
+        start_x(2, e)
 
 
     def weigh(where, rows_ref):
@@ -232,7 +232,6 @@
     def wait_sibling(cls):
         arrived(ybuf.at[cls, :, pl.ds(per_core, per_core)], ybuf_sem.at[cls])
 
-    lax.fori_loop(2, experts, functools.partial(rest_unit, load=False), 0)
 
     for cls in (0, 1):
         wait_sibling(cls)

time: 98.9 us -> 96.9 us (0.980)
  Pallas kernels: 96.9 us -> 94.9 us
    pallas_call x1, Pallas kernels: 96.9 us -> 94.9 us  [local_step(): pl.pallas_call(functools.partial(kernel, zn), out_shape=jax.ShapeDtypeStr...]
where the time goes in v4:
time: 96.9 us; the launch traced here: 96.8 us
  Pallas kernels  94.9 us (98%)
  local copies, waits for them, and re-layouts  1.88 us (2%)
    pallas_call x1, Pallas kernels, local_step(): pl.pallas_call(functools.partial(kernel, zn), out_shape=jax.ShapeDtypeStr...  94.9 us

profile of v4, /device:TPU:30, one launch (start us, length us, event | category | flops | bytes accessed | tf_op | source)
XLA Modules:
  0.0 96.8 jit_solution(10231366462095524883)
XLA Ops:
  0.0 94.9 %shard_map.82 = bf16[128,2048]{1,0:T(8,128)(2,1)} custom-call(bf16[16,4,32,2048]{3,2,1,0:T(8,128)(2,1)} %disp.1, bf16[4,2048,1024]{2,1,0:T(8,128)(2,1)} %wg.1, bf16[4,2048,1024]{2,1,0:T(8,128)(2,1)} %wu.1, bf16[4,1024,2048]{2,1,0:T(8,128)(2,1)} %wd.1, s32[4,16]{1,0:T(4,128)} %bitcast.7, s32[8,128]{1,0:T(8,128)} %bitcast.4, s32[8,128]{1,0:T(8,128)} %bitcast.5, ...), custom_call_target="tpu_custom_call" | custom-call | tf_op jit(solution)/shard_map/pallas_call | solution.py:334
  94.9 1.9 %copy.10 = bf16[128,2048]{1,0:T(8,128)(2,1)} copy(bf16[128,2048]{1,0:T(8,128)(2,1)} %shard_map.82) | data formatting | bytes 1048576
